TPU v7x, 32 devices: a whole 2x2x4 slice. The times are simulated.
32 devices in a mesh: pp: 4 (over x, core), tp: 4 (over z), dp: 2 (over y).
Axes of the slice: x: 2, y: 2, z: 4, core: 2. Of those that a mesh axis runs over, the one named last changes fastest.
Arguments:
- act_in: bfloat16 [4, 2, 128, 4096], P('pp', 'dp', 'tp'), may hold values from -6 to 6
- stash_in: bfloat16 [4, 2, 128, 4096], P('pp', 'dp', 'tp'), may hold values from -6 to 6
- grad_in: bfloat16 [4, 2, 128, 4096], P('pp', 'dp', 'tp'), may hold values from -6 to 6
- doc_ids: int32 [4, 2, 2, 128], P('pp', 'dp'), may hold values from 0 to 15, never falling along the last dimension, each value on 1 to 64 neighbouring positions
- query_weight: bfloat16 [4, 4096, 4096], P('pp', None, 'tp'), as said below
- key_weight: bfloat16 [4, 4096, 1024], P('pp', None, 'tp'), as said below
- value_weight: bfloat16 [4, 4096, 1024], P('pp', None, 'tp'), as said below
- out_weight: bfloat16 [4, 4096, 4096], P('pp', None, 'tp'), may hold values from -0.09375 to 0.09375
Outputs:
- act_out: bfloat16 [4, 2, 128, 4096], P('pp', 'dp', 'tp')
- grad_out: bfloat16 [4, 2, 128, 4096], P('pp', 'dp', 'tp')
- grad_query: float32 [4, 4096, 4096], P('pp', 'dp', 'tp')
- grad_key: float32 [4, 4096, 1024], P('pp', 'dp', 'tp')
- grad_value: float32 [4, 4096, 1024], P('pp', 'dp', 'tp')
Inputs may be any that keep to these rules, and one draw needn't show every extreme that they name: `doc_ids`: along each row of 128 positions the document numbers never fall. `query_weight`: entries of mean zero. `key_weight`: for each of the 8 key heads, its 1 stored copies (consecutive blocks of 128 columns) are equal; entries of mean zero. `value_weight`: for each of the 8 value heads, its 1 stored copies (consecutive blocks of 128 columns) are equal.
All inputs are finite; a program needn't handle non-finite values.
Results may differ from a plain program's by a relative error of at most 0.033.
Values may be sent and summed in bfloat16 or wider, within the bound.
A program may use at most 128 MiB of HBM per device.

v0:
```python
import math

import jax
import jax.numpy as jnp
from jax import lax
from jax.sharding import PartitionSpec as P

HEAD = 128


epsilon = 1e-05


def from_behind(value, axis, steps):
    count = lax.axis_size(axis)
    pairs = [(source, (source + steps) % count) for source in range(count)]
    return lax.ppermute(value, axis, pairs)


def norm_rows(token_rows):
    widened = token_rows.astype(jnp.float32)
    inverse = lax.rsqrt(jnp.mean(widened * widened, axis=-1, keepdims=True) + epsilon)
    return ((widened * inverse).astype(jnp.bfloat16), inverse)


def allowed(documents):
    length = documents.shape[0]
    position = jnp.arange(length, dtype=jnp.int32)
    return (position[None, :] <= position[:, None]) & (documents[:, None] == documents[None, :])


def project(normed, weight):
    return jnp.dot(normed, weight, preferred_element_type=jnp.float32).astype(jnp.bfloat16)


def contract_last(left_side, right_side):
    return lax.dot_general(
        left_side, right_side, (((1,), (1,)), ((), ())), preferred_element_type=jnp.float32
    )


def split_heads(queries, keys, values, kv_local):
    length = queries.shape[0]
    group_size = queries.shape[1] // (kv_local * HEAD)
    return (
        queries.reshape(length, kv_local, group_size, HEAD),
        keys.reshape(length, kv_local, HEAD),
        values.reshape(length, kv_local, HEAD),
    )


def attend_probs(query_heads, key_heads, allowed_pairs):
    scores = jnp.einsum(
        "ihgd,jhd->hgij", query_heads, key_heads, preferred_element_type=jnp.float32
    ) * (1.0 / math.sqrt(HEAD))
    scores = jnp.where(allowed_pairs, scores, -jnp.inf)
    row_max = jnp.max(scores, axis=-1, keepdims=True)
    weights = jnp.exp(scores - row_max)
    return (weights / jnp.sum(weights, axis=-1, keepdims=True)).astype(jnp.bfloat16)


def attend_back(dmixed, queries, keys, values, probs, kv_local):
    length = queries.shape[0]
    query_heads, key_heads, value_heads = split_heads(queries, keys, values, kv_local)
    dmixed_heads = dmixed.reshape(query_heads.shape)
    dprobs = jnp.einsum(
        "ihgd,jhd->hgij", dmixed_heads, value_heads, preferred_element_type=jnp.float32
    )
    weights = probs.astype(jnp.float32)
    inner = jnp.sum(weights * dprobs, axis=-1, keepdims=True)
    dscores = (weights * (dprobs - inner) * (1.0 / math.sqrt(HEAD))).astype(jnp.bfloat16)
    dqueries = jnp.einsum("hgij,jhd->ihgd", dscores, key_heads, preferred_element_type=jnp.float32)
    dkeys = jnp.einsum("hgij,ihgd->jhd", dscores, query_heads, preferred_element_type=jnp.float32)
    dvalues = jnp.einsum("hgij,ihgd->jhd", probs, dmixed_heads, preferred_element_type=jnp.float32)
    return (
        dqueries.astype(jnp.bfloat16).reshape(length, queries.shape[1]),
        dkeys.reshape(length, kv_local * HEAD),
        dvalues.reshape(length, kv_local * HEAD),
    )


def handoff(payload, offset):
    return from_behind(payload, "pp", offset)


def per_copy(left_side, right_side, copies):
    length = left_side.shape[0] // copies
    product = jnp.einsum(
        "nsd,nse->nde",
        left_side.reshape(copies, length, left_side.shape[1]),
        right_side.reshape(copies, length, right_side.shape[1]),
        preferred_element_type=jnp.float32,
    )
    kept = lax.optimization_barrier(product.astype(jnp.bfloat16))
    return jnp.sum(kept.astype(jnp.float32), axis=0)


def body(act_in, stash_in, grad_in, doc_ids, query_weight, key_weight, value_weight, out_weight):
    kv_local = key_weight.shape[2] // HEAD
    forward_rows = act_in[0, 0]
    backward_rows = stash_in[0, 0]
    grad_rows = grad_in[0, 0]
    normed_ahead, unused_inverse = norm_rows(forward_rows)
    normed_back, inverse_back = norm_rows(backward_rows)
    ahead_full, back_full, grad_full = (
        lax.all_gather(normed_ahead, "tp", axis=0, tiled=True),
        lax.all_gather(normed_back, "tp", axis=0, tiled=True),
        lax.all_gather(grad_rows, "tp", axis=0, tiled=True),
    )
    w_query = query_weight[0]
    w_key = key_weight[0]
    w_value = value_weight[0]
    w_out = out_weight[0]
    queries_ahead = project(ahead_full, w_query)
    keys_ahead = project(ahead_full, w_key)
    values_ahead = project(ahead_full, w_value)
    query_heads, key_heads, value_heads = split_heads(
        queries_ahead, keys_ahead, values_ahead, kv_local
    )
    probs_ahead = attend_probs(query_heads, key_heads, allowed(doc_ids[0, 0, 0]))
    mixed_ahead = jnp.einsum(
        "hgij,jhd->ihgd", probs_ahead, value_heads, preferred_element_type=jnp.float32
    )
    mixed_ahead = mixed_ahead.astype(jnp.bfloat16).reshape(queries_ahead.shape)
    forward_sum = contract_last(mixed_ahead, w_out)
    queries_back = project(back_full, w_query)
    keys_back = project(back_full, w_key)
    values_back = project(back_full, w_value)
    query_back_heads, key_back_heads, unused_values = split_heads(
        queries_back, keys_back, values_back, kv_local
    )
    probs_back = attend_probs(query_back_heads, key_back_heads, allowed(doc_ids[0, 0, 1]))
    dmixed = jnp.dot(grad_full, w_out, preferred_element_type=jnp.float32).astype(jnp.bfloat16)
    dqueries, dkeys, dvalues = attend_back(
        dmixed, queries_back, keys_back, values_back, probs_back, kv_local
    )
    dkey_cols = dkeys.astype(jnp.bfloat16)
    dvalue_cols = dvalues.astype(jnp.bfloat16)
    dnormed = (
        contract_last(dqueries, w_query)
        + contract_last(dkey_cols, w_key)
        + contract_last(dvalue_cols, w_value)
    )
    forward_share, backward_share = (
        lax.psum_scatter(
            forward_sum.astype(jnp.bfloat16), "tp", scatter_dimension=0, tiled=True
        ).astype(jnp.float32),
        lax.psum_scatter(
            dnormed.astype(jnp.bfloat16), "tp", scatter_dimension=0, tiled=True
        ).astype(jnp.float32),
    )
    outgoing = (forward_rows.astype(jnp.float32) + forward_share).astype(jnp.bfloat16)
    scaled = backward_rows.astype(jnp.float32) * inverse_back
    grad_back = (
        grad_rows.astype(jnp.float32)
        + inverse_back
        * (backward_share - scaled * jnp.mean(backward_share * scaled, axis=-1, keepdims=True))
    ).astype(jnp.bfloat16)
    act_out = handoff(outgoing, 1)[None, None]
    grad_out = handoff(grad_back, -1)[None, None]
    copies = lax.axis_size("dp")
    normed_cols = lax.all_to_all(back_full, "dp", split_axis=1, concat_axis=0, tiled=True)
    all_queries, all_keys, all_values = (
        lax.all_gather(dqueries, "dp", axis=0, tiled=True),
        lax.all_gather(dkey_cols, "dp", axis=0, tiled=True),
        lax.all_gather(dvalue_cols, "dp", axis=0, tiled=True),
    )
    grad_query = per_copy(normed_cols, all_queries, copies)[None]
    grad_key = per_copy(normed_cols, all_keys, copies)[None]
    grad_value = per_copy(normed_cols, all_values, copies)[None]
    return (act_out, grad_out, grad_query, grad_key, grad_value)


def solution(mesh):
    placed = (
        P("pp", "dp", "tp", None),
        P("pp", "dp", "tp", None),
        P("pp", "dp", "tp", None),
        P("pp", "dp", None, None),
        P("pp", None, "tp"),
        P("pp", None, "tp"),
        P("pp", None, "tp"),
        P("pp", None, "tp"),
    )
    return jax.shard_map(
        body,
        mesh=mesh,
        in_specs=placed,
        out_specs=(
            P("pp", "dp", "tp", None),
            P("pp", "dp", "tp", None),
            P("pp", "dp", "tp"),
            P("pp", "dp", "tp"),
            P("pp", "dp", "tp"),
        ),
        check_vma=False,
    )
```

profile of v0, /device:TPU:1, one launch (start us, length us, event | category | flops | bytes accessed | tf_op | source)
XLA Modules:
  0.0 207.6 jit_solution(1931874249272098279)
XLA Ops:
  15.4 25.2 %all-gather.7.cloned.1.call-done = bf16[128,4096]{1,0:T(8,128)(2,1)} async-done(((bf16[32,4096]{1,0:T(8,128)(2,1)}), bf16[128,4096]{1,0:T(8,128)(2,1)}) %all-gather.7.cloned.1.call-update) | async-done | bytes 1048592 | tf_op jit(solution)/shard_map/all_gather | solution.py:107
  40.6 5.0 %fusion.42 = bf16[128,1024]{1,0:T(8,128)(2,1)S(1)} fusion(bf16[128,4096]{1,0:T(8,128)(2,1)} %all-gather.7.cloned.1.call-done, bf16[1,4096,1024]{2,1,0:T(8,128)(2,1)} %param.12), kind=kOutput, calls=%fused_computation.49 | convolution fusion | flops 1073872896 | bytes 9699328 | tf_op jit(solution)/shard_map/dot_general | solution.py:33
  47.1 2.0 fusion.51
  49.2 20.4 %all-gather.9.cloned.1.call-done = bf16[1,1,128,4096]{3,2,1,0:T(8,128)(2,1)} async-done(((bf16[1,1,32,4096]{3,2,1,0:T(8,128)(2,1)}), bf16[1,1,128,4096]{3,2,1,0:T(8,128)(2,1)}) %all-gather.9.cloned.1.call-update) | async-done | bytes 1048592 | tf_op jit(solution)/shard_map/all_gather | solution.py:108
  69.6 5.7 %fusion.45 = bf16[128,1024]{1,0:T(8,128)(2,1)} fusion(bf16[1,4096,1024]{2,1,0:T(8,128)(2,1)} %param.15, bf16[1,1,128,4096]{3,2,1,0:T(8,128)(2,1)} %all-gather.9.cloned.1.call-done), kind=kOutput, calls=%fused_computation.50 | convolution fusion | flops 1073872896 | bytes 9699328 | tf_op jit(solution)/shard_map/dot_general | solution.py:133
  76.4 2.7 %fusion.111 = (f32[2,4,128]{2,1,0:T(4,128)}, f32[2,4,128,128]{2,3,1,0:T(8,128)}) fusion(bf16[128,2,128,1]{0,2,3,1:T(8,128)(2,1)S(1)} %copy.36, bf16[128,2,4,128]{0,3,2,1:T(8,128)(2,1)} %bitcast.170, pred[128,128]{0,1:T(8,128)(4,1)} %fusion.90), kind=kOutput, calls=%fused_computation.113 | convolution fusion | flops 34078848 | bytes 872448 | tf_op jit(solution)/shard_map/sub | solution.py:58
  81.9 2.5 %convolution_convert_fusion.3 = bf16[2,128,4,128]{3,1,2,0:T(8,128)(2,1)} fusion(bf16[128,2,128,1]{0,2,3,1:T(8,128)(2,1)S(1)} %copy.36, f32[2,4,128,128]{2,3,1,0:T(8,128)} %convolution_bitcast_fusion, bf16[2,4,128,128]{2,3,1,0:T(8,128)(2,1)} %divide_convert_fusion), kind=kOutput, calls=%fused_computation.51 | convolution fusion | flops 34604160 | bytes 1114112 | tf_op jit(solution)/shard_map/hgij,jhd->ihgd/dot_general | solution.py:72
  84.4 2.4 %fusion.60 = bf16[2,128,128]{2,1,0:T(8,128)(2,1)} fusion(bf16[128,2,4,128]{0,3,2,1:T(8,128)(2,1)} %bitcast.171, f32[2,4,128,128]{2,3,1,0:T(8,128)} %convolution_bitcast_fusion, bf16[2,4,128,128]{2,3,1,0:T(8,128)(2,1)} %divide_convert_fusion), kind=kOutput, calls=%fused_computation.59 | convolution fusion | flops 34505856 | bytes 1114112 | tf_op jit(solution)/shard_map/hgij,ihgd->jhd/dot_general | solution.py:73
  86.9 9.4 %all_gather.21 = bf16[256,1024]{0,1:T(8,128)(2,1)} all-gather(bf16[128,1024]{0,1:T(8,128)(2,1)} %bitcast.161), channel_id=1, replica_groups=mesh['pp'=4,'tp'=4,'dp'=2] {'dp'}, dimensions={0}, use_global_device_ids=true | all-gather | bytes 786432 | tf_op jit(solution)/shard_map/all_gather | solution.py:164
  96.2 2.0 copy.28
  99.6 3.6 %all-to-all-start = ((bf16[128,2,2048]{0,2,1:T(8,128)(2,1)}), bf16[128,2,2048]{0,2,1:T(8,128)(2,1)S(1)}, u32[]{:S(2)}, u32[]{:S(2)}) async-start(bf16[128,2,2048]{0,2,1:T(8,128)(2,1)} %bitcast.155), calls=%async_computation.2 | async-start | bytes 2097152 | tf_op jit(solution)/shard_map/all_to_all | solution.py:162
  103.2 13.3 %all_gather.22 = bf16[256,256]{0,1:T(8,128)(2,1)S(1)} all-gather(bf16[128,256]{0,1:T(8,128)(2,1)} %bitcast.167), channel_id=1, replica_groups=mesh['pp'=4,'tp'=4,'dp'=2] {'dp'}, dimensions={0}, use_global_device_ids=true | all-gather | bytes 196608 | tf_op jit(solution)/shard_map/all_gather | solution.py:165
  118.5 3.8 %all_gather.23 = bf16[256,256]{0,1:T(8,128)(2,1)S(1)} all-gather(bf16[128,256]{0,1:T(8,128)(2,1)S(1)} %bitcast.163), channel_id=1, replica_groups=mesh['pp'=4,'tp'=4,'dp'=2] {'dp'}, dimensions={0}, use_global_device_ids=true | all-gather | bytes 196608 | tf_op jit(solution)/shard_map/all_gather | solution.py:166
  123.0 6.4 %fusion.7 = f32[128,4096]{1,0:T(8,128)S(1)} fusion(bf16[128,1024]{0,1:T(8,128)(2,1)} %bitcast.162, bf16[1,4096,1024]{2,1,0:T(8,128)(2,1)} %param.12), kind=kOutput, calls=%fused_computation.8 | convolution fusion | flops 1073741824 | bytes 10747904 | tf_op jit(solution)/shard_map/dot_general | solution.py:37
  133.2 5.0 %fusion.39 = bf16[128,1024]{1,0:T(8,128)(2,1)S(1)} fusion(bf16[128,4096]{1,0:T(8,128)(2,1)} %all-gather.5.cloned.1.call-done, bf16[1,4096,1024]{2,1,0:T(8,128)(2,1)} %param.12), kind=kOutput, calls=%fused_computation.48 | convolution fusion | flops 1073872896 | bytes 9699328 | tf_op jit(solution)/shard_map/dot_general | solution.py:33
  140.7 2.6 %fusion.48 = bf16[128,256]{1,0:T(8,128)(2,1)S(1)} fusion(bf16[128,4096]{1,0:T(8,128)(2,1)} %all-gather.5.cloned.1.call-done, bf16[1,4096,256]{2,1,0:T(8,128)(2,1)} %param.14), kind=kOutput, calls=%fused_computation.55 | convolution fusion | flops 268468224 | bytes 3211264 | tf_op jit(solution)/shard_map/dot_general | solution.py:33
  147.5 7.3 %fusion.14 = bf16[128,4096]{1,0:T(8,128)(2,1)} fusion(bf16[128,1024]{0,1:T(8,128)(2,1)S(1)} %bitcast.169, bf16[1,4096,1024]{2,1,0:T(8,128)(2,1)} %param.15), kind=kOutput, calls=%fused_computation.18 | convolution fusion | flops 1074266112 | bytes 9699328 | tf_op jit(solution)/shard_map/dot_general | solution.py:37
  154.9 6.6 %convolution_convert_fusion = bf16[2,2048,1024]{2,1,0:T(8,128)(2,1)} fusion(bf16[2,128,1024]{2,1,0:T(8,128)(2,1)} %bitcast.158, bf16[128,2,2048]{0,2,1:T(8,128)(2,1)S(1)} %all-to-all-done), kind=kOutput, calls=%fused_computation.14 | convolution fusion | flops 1077936128 | bytes 9961472 | tf_op jit(solution)/shard_map/nsd,nse->nde/dot_general | solution.py:88
  163.5 2.1 %convolution_convert_fusion.1 = bf16[2,2048,256]{2,1,0:T(8,128)(2,1)} fusion(bf16[2,128,256]{2,1,0:T(8,128)(2,1)S(1)} %bitcast.166, bf16[128,2,2048]{0,2,1:T(8,128)(2,1)S(1)} %all-to-all-done), kind=kOutput, calls=%fused_computation.21 | convolution fusion | flops 269484032 | bytes 3276800 | tf_op jit(solution)/shard_map/nsd,nse->nde/dot_general | solution.py:88
  165.6 10.0 %convert_reduce_fusion = f32[2048,1024]{1,0:T(8,128)} fusion(bf16[2,2048,1024]{2,1,0:T(8,128)(2,1)} %convolution_convert_fusion), kind=kLoop, calls=%fused_computation.3 | loop fusion | flops 6291456 | bytes 16777216 | tf_op jit(solution)/shard_map/reduce_sum | solution.py:95
  178.0 3.9 %collective-permute-start.1 = (bf16[32,4096]{1,0:T(8,128)(2,1)S(1)}, bf16[32,4096]{1,0:T(8,128)(2,1)S(1)}, u32[]{:S(2)}, u32[]{:S(2)}) collective-permute-start(bf16[32,4096]{1,0:T(8,128)(2,1)S(1)} %fusion.79), channel_id=1, source_target_pairs={{0,24},{8,0},{16,8},{24,16},{1,25},{9,1},{17,9},{25,17},{2,26},{10... | collective-permute-start | bytes 786440 | tf_op jit(solution)/shard_map/ppermute | solution.py:17
  181.9 9.3 %reduce-scatter.3.cloned.1.call-done = bf16[32,4096]{1,0:T(8,128)(2,1)} async-done(((bf16[128,4096]{1,0:T(8,128)(2,1)}), bf16[32,4096]{1,0:T(8,128)(2,1)}) %reduce-scatter.3.cloned.1.call-update) | async-done | bytes 262160 | tf_op jit(solution)/shard_map/reduce_scatter | solution.py:145
  192.2 2.2 %collective-permute-start = (bf16[32,4096]{1,0:T(8,128)(2,1)S(1)}, bf16[32,4096]{1,0:T(8,128)(2,1)S(1)}, u32[]{:S(2)}, u32[]{:S(2)}) collective-permute-start(bf16[32,4096]{1,0:T(8,128)(2,1)S(1)} %fusion.84), channel_id=1, source_target_pairs={{0,8},{8,16},{16,24},{24,0},{1,9},{9,17},{17,25},{25,1},{2,10},{10... | collective-permute-start | bytes 786440 | tf_op jit(solution)/shard_map/ppermute | solution.py:17
  194.4 3.5 %convert_reduce_fusion.2 = f32[2048,256]{1,0:T(8,128)} fusion(bf16[2,2048,256]{2,1,0:T(8,128)(2,1)} %convolution_convert_fusion.2), kind=kLoop, calls=%fused_computation.20 | loop fusion | flops 1572864 | bytes 4194304 | tf_op jit(solution)/shard_map/reduce_sum | solution.py:95
  (83 shorter events, 36.6 us)
Async XLA Ops:
  7.2 39.3 %copy-start = (bf16[1,4096,256]{2,1,0:T(8,128)(2,1)S(1)}, bf16[1,4096,256]{2,1,0:T(8,128)(2,1)}, u32[]{:S(2)}) copy-start(bf16[1,4096,256]{2,1,0:T(8,128)(2,1)} %param.13) | copy-start | bytes 6291460
  7.2 7.4 %copy-start.14 = (s32[1,1,2,128]{3,2,1,0:T(2,128)S(1)}, s32[1,1,2,128]{3,2,1,0:T(2,128)}, u32[]{:S(2)}) copy-start(s32[1,1,2,128]{3,2,1,0:T(2,128)} %param.11) | copy-start | bytes 3076
  7.2 33.4 %all-gather.7.cloned.1.call-start = ((), (), s32[]{:S(2)}) async-start(), calls=%async_computation.5 | async-start | bytes 1310720 | tf_op jit(solution)/shard_map/all_gather | solution.py:107
  8.5 0.6 copy-start.12
  10.9 58.7 %all-gather.9.cloned.1.call-start = ((), (), s32[]{:S(2)}) async-start(), calls=%async_computation.7 | async-start | bytes 1310720 | tf_op jit(solution)/shard_map/all_gather | solution.py:108
  11.6 121.5 %all-gather.5.cloned.1.call-start = ((), (), s32[]{:S(2)}) async-start(), calls=%async_computation.3 | async-start | bytes 1310720 | tf_op jit(solution)/shard_map/all_gather | solution.py:106
  40.6 5.9 %copy-start.1 = (bf16[128,4096]{1,0:T(8,128)(2,1)S(1)}, bf16[128,4096]{1,0:T(8,128)(2,1)}, u32[]{:S(2)}) copy-start(bf16[128,4096]{1,0:T(8,128)(2,1)} %all-gather.7.cloned.1.call-done) | copy-start | bytes 3145732
  99.6 55.3 %all-to-all-start = ((bf16[128,2,2048]{0,2,1:T(8,128)(2,1)}), bf16[128,2,2048]{0,2,1:T(8,128)(2,1)S(1)}, u32[]{:S(2)}, u32[]{:S(2)}) async-start(bf16[128,2,2048]{0,2,1:T(8,128)(2,1)} %bitcast.155), calls=%async_computation.2 | async-start | bytes 2097152 | tf_op jit(solution)/shard_map/all_to_all | solution.py:162
  103.2 72.5 %reduce-scatter.5.cloned.1.call-start = ((), (), s32[]{:S(2)}) async-start(), calls=%async_computation.6 | async-start | bytes 1310720 | tf_op jit(solution)/shard_map/reduce_scatter | solution.py:148
  123.0 6.4 %copy-start.10 = (bf16[2,128,128]{2,1,0:T(8,128)(2,1)S(1)}, bf16[2,128,128]{2,1,0:T(8,128)(2,1)}, u32[]{:S(2)}) copy-start(bf16[2,128,128]{2,1,0:T(8,128)(2,1)} %fusion.60) | copy-start | bytes 196612
  129.5 1.6 copy-start.2
  132.9 58.3 %reduce-scatter.3.cloned.1.call-start = ((), (), s32[]{:S(2)}) async-start(), calls=%async_computation.4 | async-start | bytes 1310720 | tf_op jit(solution)/shard_map/reduce_scatter | solution.py:145
  140.7 3.3 %copy-start.7 = (bf16[128,2,4,128]{3,2,1,0:T(4,128)(2,1)S(1)}, bf16[128,2,4,128]{3,2,1,0:T(4,128)(2,1)}, u32[]{:S(2)}) copy-start(bf16[128,2,4,128]{3,2,1,0:T(4,128)(2,1)} %reshape.96) | copy-start | bytes 786436
  144.0 2.0 copy-start.11
  154.8 6.6 %copy-start.8 = (bf16[256,256]{1,0:T(8,128)(2,1)S(1)}, bf16[256,256]{1,0:T(8,128)(2,1)}, u32[]{:S(2)}) copy-start(bf16[256,256]{1,0:T(8,128)(2,1)} %copy.29) | copy-start | bytes 393220
  161.5 2.0 copy-start.9
  165.6 10.0 %copy-start.4 = (bf16[1,1,32,4096]{3,2,1,0:T(8,128)(2,1)S(1)}, bf16[1,1,32,4096]{3,2,1,0:T(8,128)(2,1)}, u32[]{:S(2)}) copy-start(bf16[1,1,32,4096]{3,2,1,0:T(8,128)(2,1)} %param.9) | copy-start | bytes 786436
  165.6 10.0 %copy-start.13 = (f32[32]{0:T(128)S(1)}, f32[32]{0:T(128)}, u32[]{:S(2)}) copy-start(f32[32]{0:T(128)} %copy-done.12) | copy-start | bytes 388
  165.6 11.3 %copy-start.6 = (bf16[1,1,32,4096]{3,2,1,0:T(8,128)(2,1)S(1)}, bf16[1,1,32,4096]{3,2,1,0:T(8,128)(2,1)}, u32[]{:S(2)}) copy-start(bf16[1,1,32,4096]{3,2,1,0:T(8,128)(2,1)} %param.10) | copy-start | bytes 786436
  165.6 25.6 %copy-start.5 = (bf16[1,1,32,4096]{3,2,1,0:T(8,128)(2,1)S(1)}, bf16[1,1,32,4096]{3,2,1,0:T(8,128)(2,1)}, u32[]{:S(2)}) copy-start(bf16[1,1,32,4096]{3,2,1,0:T(8,128)(2,1)} %param.8) | copy-start | bytes 786436
  178.0 21.6 %collective-permute-start.1 = (bf16[32,4096]{1,0:T(8,128)(2,1)S(1)}, bf16[32,4096]{1,0:T(8,128)(2,1)S(1)}, u32[]{:S(2)}, u32[]{:S(2)}) collective-permute-start(bf16[32,4096]{1,0:T(8,128)(2,1)S(1)} %fusion.79), channel_id=1, source_target_pairs={{0,24},{8,0},{16,8},{24,16},{1,25},{9,1},{17,9},{25,17},{2,26},{10... | collective-permute-start | bytes 786440 | tf_op jit(solution)/shard_map/ppermute | solution.py:17
  192.2 5.7 %copy-start.3 = (bf16[2,2048,256]{2,1,0:T(8,128)(2,1)S(1)}, bf16[2,2048,256]{2,1,0:T(8,128)(2,1)}, u32[]{:S(2)}) copy-start(bf16[2,2048,256]{2,1,0:T(8,128)(2,1)} %convolution_convert_fusion.1) | copy-start | bytes 6291460
  192.2 7.4 %collective-permute-start = (bf16[32,4096]{1,0:T(8,128)(2,1)S(1)}, bf16[32,4096]{1,0:T(8,128)(2,1)S(1)}, u32[]{:S(2)}, u32[]{:S(2)}) collective-permute-start(bf16[32,4096]{1,0:T(8,128)(2,1)S(1)} %fusion.84), channel_id=1, source_target_pairs={{0,8},{8,16},{16,24},{24,0},{1,9},{9,17},{17,25},{25,1},{2,10},{10... | collective-permute-start | bytes 786440 | tf_op jit(solution)/shard_map/ppermute | solution.py:17
Sparse Core Ops, SparseCore 0:
  11.0 29.5 all-gather.6
  42.2 27.4 all-gather.8
  71.8 27.2 all-gather.4
  133.0 29.5 reduce-scatter.4
  165.4 25.7 reduce-scatter.2
where the time goes:
time: 209 us; the launch traced here: 208 us
  matrix products  62.8 us (30%)
  waiting for transfers between devices  55.7 us (27%)
  other arithmetic  27.1 us (13%)
  blocking collectives  26.5 us (13%)
  between operations  14 us (7%)
  local copies, waits for them, and re-layouts  11.4 us (5%)
  starting transfers between devices  10 us (5%)
    all_gather x1, waiting for transfers between devices, body(): lax.all_gather(normed_back, 'tp', axis=0, tiled=True)  25.2 us
    all_gather x1, waiting for transfers between devices, body(): lax.all_gather(grad_rows, 'tp', axis=0, tiled=True)  20.4 us
    dot_general x6, matrix products, project(): jnp.dot(normed, weight, preferred_element_type=jnp.float32)  16.7 us
    dot_general x4, matrix products, contract_last(): lax.dot_general(left_side, right_side, (((1,), (1,)), ((), ())), preferre...  16.4 us
    reduce_sum x3, other arithmetic, per_copy(): return jnp.sum(kept.astype(jnp.float32), axis=0)  15.2 us
    all_gather x1, blocking collectives, body(): lax.all_gather(dkey_cols, 'dp', axis=0, tiled=True)  13.3 us
    dot_general x3, matrix products, per_copy(): jnp.einsum('nsd,nse->nde', left_side.reshape(copies, length, left_side.sh...  10.7 us
    all_gather x1, blocking collectives, body(): lax.all_gather(dqueries, 'dp', axis=0, tiled=True)  9.38 us
  transfers between devices with their start and end apart: 8, of which 3 were waited for; matrix products, arithmetic and copies ran while one was open for 46% of the time, Pallas kernels for 0%

commit v1 on v0

--- a/solution.py
+++ b/solution.py
@@ -1,8 +1,11 @@
+import functools
 import math
 
 import jax
 import jax.numpy as jnp
 from jax import lax
+from jax.experimental import pallas as pl
+from jax.experimental.pallas import tpu as pltpu
 from jax.sharding import PartitionSpec as P
 
 HEAD = 128
@@ -17,6 +20,341 @@
     return lax.ppermute(value, axis, pairs)
 
 
+MESH = pl.DeviceIdType.MESH
+VMEM_LIMIT = 60 * 1024 * 1024
+
+
+def remote(source, target, send_sem, recv_sem, axis, device):
+    return pltpu.make_async_remote_copy(
+        src_ref=source,
+        dst_ref=target,
+        send_sem=send_sem,
+        recv_sem=recv_sem,
+        device_id={axis: device},
+        device_id_type=MESH,
+    )
+
+
+def greet(n, copies, me, mine):
+    barrier = pltpu.get_barrier_semaphore()
+
+    @pl.when(me > 0)
+    def _():
+        pl.semaphore_signal(barrier, inc=1, device_id={"tp": me - 1}, device_id_type=MESH)
+
+    @pl.when(me < n - 1)
+    def _():
+        pl.semaphore_signal(barrier, inc=1, device_id={"tp": me + 1}, device_id_type=MESH)
+
+    for offset in range(1, copies):
+        other = lax.rem(mine + offset, copies)
+        pl.semaphore_signal(barrier, inc=1, device_id={"dp": other}, device_id_type=MESH)
+
+    ends = jnp.where(me > 0, 1, 0) + jnp.where(me < n - 1, 1, 0)
+    pl.semaphore_wait(barrier, ends + copies - 1)
+
+
+def gather_kernel(
+    n, copies,
+    act, stash, grad, wq, wk, wv, wo,
+    qb, kb, vb, qf, kf, vf, dm, ncols,
+    full, normed, vq, vk, vv, vo, wsem, ss, rs, dss, drs,
+):
+    me = lax.axis_index("tp")
+    mine = lax.axis_index("dp")
+    rows, width = act.shape
+    piece = width // copies
+    loads = []
+    for i, (hbm, vmem) in enumerate(((wq, vq), (wk, vk), (wv, vv), (wo, vo))):
+        load = pltpu.make_async_copy(hbm, vmem, wsem.at[i])
+        load.start()
+        loads.append(load)
+    greet(n, copies, me, mine)
+    own = (act, stash, grad)
+
+    def block(a, index):
+        return full.at[a, pl.ds(pl.multiple_of(index * rows, rows), rows), :]
+
+    def hop(a, side, step):
+        toward = 1 if side == 0 else -1
+        carried = me - toward * (step - 1)
+        source = own[a] if step == 1 else block(a, carried)
+        return remote(
+            source, block(a, carried),
+            ss.at[a, side, step - 1], rs.at[a, side, step - 1], "tp", me + toward,
+        )
+
+    def sends(side, step):
+        if side == 0:
+            return (me < n - 1) & (me - (step - 1) >= 0)
+        return (me > 0) & (me + (step - 1) < n)
+
+    def gets(side, step):
+        return (me - step >= 0) if side == 0 else (me + step < n)
+
+    def start(a, step):
+        for side in range(2):
+            @pl.when(sends(side, step))
+            def _():
+                hop(a, side, step).start()
+
+    def arrive(a, step):
+        for side in range(2):
+            @pl.when(gets(side, step))
+            def _():
+                toward = 1 if side == 0 else -1
+                landed = block(a, me - toward * step)
+                remote(
+                    landed, landed,
+                    ss.at[a, side, step - 1], rs.at[a, side, step - 1], "tp",
+                    jnp.where(me == 0, 1, me - 1),
+                ).wait_recv()
+
+            if step < n - 1:
+                @pl.when(sends(side, step + 1))
+                def _():
+                    hop(a, side, step + 1).start()
+
+    def place(a):
+        full[a, pl.ds(pl.multiple_of(me * rows, rows), rows), :] = own[a][...]
+
+    def multiply(left, right, out):
+        tile = 256
+
+        @pl.loop(0, right.shape[1] // tile)
+        def _(t):
+            columns = pl.ds(pl.multiple_of(t * tile, tile), tile)
+            out[:, columns] = jnp.dot(
+                left[...], right[:, columns], preferred_element_type=jnp.float32
+            ).astype(jnp.bfloat16)
+
+    def normalise(a):
+        band = 16
+
+        @pl.loop(0, full.shape[1] // band)
+        def _(t):
+            where = pl.ds(pl.multiple_of(t * band, band), band)
+            wide = full[a, where, :].astype(jnp.float32)
+            inverse = lax.rsqrt(jnp.mean(wide * wide, axis=-1, keepdims=True) + epsilon)
+            normed[where, :] = (wide * inverse).astype(jnp.bfloat16)
+
+    start(0, 1)
+    start(1, 1)
+    for a in range(3):
+        place(a)
+    for step in range(1, n):
+        arrive(0, step)
+    start(2, 1)
+    arrive(1, 1)
+    normalise(0)
+    for load in loads:
+        load.wait()
+    multiply(normed, vq, qb)
+    multiply(normed, vk, kb)
+    multiply(normed, vv, vb)
+    trades = []
+    for offset in range(1, copies):
+        other = lax.rem(mine + offset, copies)
+        trade = remote(
+            normed.at[:, pl.ds(pl.multiple_of(other * piece, piece), piece)],
+            ncols.at[mine], dss.at[offset], drs.at[offset], "dp", other,
+        )
+        trade.start()
+        trades.append(trade)
+    ncols[mine] = normed[:, pl.ds(pl.multiple_of(mine * piece, piece), piece)]
+    for step in range(2, n):
+        arrive(1, step)
+    arrive(2, 1)
+    multiply(full.at[1], vo, dm)
+    for step in range(2, n):
+        arrive(2, step)
+    for trade in trades:
+        trade.wait()
+    normalise(2)
+    multiply(normed, vq, qf)
+    multiply(normed, vk, kf)
+    multiply(normed, vv, vf)
+    for a in range(3):
+        for step in range(1, n):
+            for side in range(2):
+                @pl.when(sends(side, step))
+                def _():
+                    hop(a, side, step).wait_send()
+
+
+def gather_call(n, copies, act, grad, stash, wq, wk, wv, wo):
+    rows, width = act.shape
+    seq = rows * n
+    bf = jnp.bfloat16
+    vmem = pl.BlockSpec(memory_space=pltpu.VMEM)
+    anywhere = pl.BlockSpec(memory_space=pl.ANY)
+    shapes = [(seq, w.shape[1]) for w in (wq, wk, wv)] * 2 + [(seq, wo.shape[1])]
+    shapes += [(copies, seq, width // copies)]
+    sem = pltpu.SemaphoreType.DMA
+    return pl.pallas_call(
+        functools.partial(gather_kernel, n, copies),
+        out_shape=[jax.ShapeDtypeStruct(shape, bf) for shape in shapes],
+        in_specs=[vmem] * 3 + [anywhere] * 4,
+        out_specs=[vmem] * len(shapes),
+        scratch_shapes=[pltpu.VMEM((3, seq, width), bf), pltpu.VMEM((seq, width), bf)]
+        + [pltpu.VMEM(w.shape, bf) for w in (wq, wk, wv, wo)]
+        + [sem((4,)), sem((3, 2, n)), sem((3, 2, n)), sem((copies,)), sem((copies,))],
+        compiler_params=pltpu.CompilerParams(
+            collective_id=0, has_side_effects=True, vmem_limit_bytes=VMEM_LIMIT
+        ),
+        cost_estimate=pl.CostEstimate(
+            flops=40_000_000_000, bytes_accessed=30_000_000, transcendentals=0
+        ),
+    )(stash, grad, act, wq, wk, wv, wo)
+
+
+def scatter_kernel(
+    n, copies,
+    fsum, bsum, dq, dk, dv,
+    fshare, bshare, aq, ak, av,
+    slots, ss, rs, dss, drs,
+):
+    me = lax.axis_index("tp")
+    mine = lax.axis_index("dp")
+    rows, width = fshare.shape
+    sums = (bsum, fsum)
+    greet(n, copies, me, mine)
+    trades = []
+    for offset in range(1, copies):
+        other = lax.rem(mine + offset, copies)
+        for i, (source, target) in enumerate(((dq, aq), (dk, ak), (dv, av))):
+            trade = remote(
+                source, target.at[mine], dss.at[offset, i], drs.at[offset, i], "dp", other
+            )
+            trade.start()
+            trades.append(trade)
+
+    def copy(a, side, dest, first):
+        toward = 1 if side == 0 else -1
+        part = sums[a].at[pl.ds(dest * rows, rows), :]
+        return remote(
+            part if first else slots.at[a, side, dest], slots.at[a, side, dest],
+            ss.at[a, side, dest], rs.at[a, side, dest], "tp", me + toward,
+        )
+
+    def landed(a, side, dest):
+        slot = slots.at[a, side, dest]
+        remote(
+            slot, slot, ss.at[a, side, dest], rs.at[a, side, dest], "tp",
+            jnp.where(me == 0, 1, me - 1),
+        ).wait_recv()
+
+    def roles(side, dest):
+        if side == 0:
+            return me == 0, (me > 0) & (me < dest)
+        return me == n - 1, (me < n - 1) & (me > dest)
+
+    routes = []
+    for k in range(n - 1):
+        for side in range(2):
+            routes.append((side, n - 1 - k if side == 0 else k))
+    for a in range(2):
+        for side, dest in routes:
+            first, middle = roles(side, dest)
+
+            @pl.when(first)
+            def _():
+                copy(a, side, dest, True).start()
+
+    aq[mine] = dq[...]
+    ak[mine] = dk[...]
+    av[mine] = dv[...]
+    for a in range(2):
+        for side, dest in routes:
+            first, middle = roles(side, dest)
+
+            @pl.when(middle)
+            def _():
+                landed(a, side, dest)
+                slots[a, side, dest] = (
+                    slots[a, side, dest].astype(jnp.float32)
+                    + sums[a][dest * rows : (dest + 1) * rows, :].astype(jnp.float32)
+                ).astype(jnp.bfloat16)
+                copy(a, side, dest, False).start()
+
+    for a, out in enumerate((bshare, fshare)):
+        out[...] = sums[a][pl.ds(pl.multiple_of(me * rows, rows), rows), :].astype(jnp.float32)
+        for side, dest in routes:
+            @pl.when(me == dest)
+            def _():
+                landed(a, side, dest)
+                out[...] += slots[a, side, dest].astype(jnp.float32)
+
+    for a in range(2):
+        for side, dest in routes:
+            first, middle = roles(side, dest)
+
+            @pl.when(first | middle)
+            def _():
+                copy(a, side, dest, False).wait_send()
+
+    for trade in trades:
+        trade.wait()
+
+
+def scatter_call(n, copies, fsum, bsum, dq, dk, dv):
+    seq, width = fsum.shape
+    rows = seq // n
+    vmem = pl.BlockSpec(memory_space=pltpu.VMEM)
+    sem = pltpu.SemaphoreType.DMA
+    return pl.pallas_call(
+        functools.partial(scatter_kernel, n, copies),
+        out_shape=[jax.ShapeDtypeStruct((rows, width), jnp.float32)] * 2
+        + [jax.ShapeDtypeStruct((copies,) + g.shape, jnp.bfloat16) for g in (dq, dk, dv)],
+        in_specs=[vmem] * 5,
+        out_specs=[vmem] * 5,
+        scratch_shapes=[
+            pltpu.VMEM((2, 2, n, rows, width), jnp.bfloat16),
+            sem((2, 2, n)), sem((2, 2, n)), sem((copies, 3)), sem((copies, 3)),
+        ],
+        compiler_params=pltpu.CompilerParams(
+            collective_id=1, has_side_effects=True, vmem_limit_bytes=40 * 1024 * 1024
+        ),
+        cost_estimate=pl.CostEstimate(
+            flops=30_000_000_000, bytes_accessed=10_000_000, transcendentals=0
+        ),
+    )(fsum, bsum, dq, dk, dv)
+
+
+def weights_kernel(copies, ncols, aq, ak, av, gq, gk, gv):
+    for right, out in ((aq, gq), (ak, gk), (av, gv)):
+        total = None
+        for i in range(copies):
+            term = lax.dot_general(
+                ncols[i], right[i], (((0,), (0,)), ((), ())),
+                preferred_element_type=jnp.float32,
+            ).astype(jnp.bfloat16).astype(jnp.float32)
+            total = term if total is None else total + term
+        out[...] = total
+
+
+def weights_call(ncols, aq, ak, av):
+    copies, seq, piece = ncols.shape
+    tile = min(256, piece)
+    whole = [
+        pl.BlockSpec(g.shape, lambda t: (0, 0, 0)) for g in (aq, ak, av)
+    ]
+    outs = [jax.ShapeDtypeStruct((piece, g.shape[2]), jnp.float32) for g in (aq, ak, av)]
+    return pl.pallas_call(
+        functools.partial(weights_kernel, copies),
+        grid=(piece // tile,),
+        out_shape=outs,
+        in_specs=[pl.BlockSpec((copies, seq, tile), lambda t: (0, 0, t))] + whole,
+        out_specs=[pl.BlockSpec((tile, o.shape[1]), lambda t: (t, 0)) for o in outs],
+        compiler_params=pltpu.CompilerParams(vmem_limit_bytes=40 * 1024 * 1024),
+        cost_estimate=pl.CostEstimate(
+            flops=2 * copies * seq * piece * sum(o.shape[1] for o in outs),
+            bytes_accessed=4 * piece * sum(o.shape[1] for o in outs),
+            transcendentals=0,
+        ),
+    )(ncols, aq, ak, av)
+
+
 def norm_rows(token_rows):
     widened = token_rows.astype(jnp.float32)
     inverse = lax.rsqrt(jnp.mean(widened * widened, axis=-1, keepdims=True) + epsilon)
@@ -27,10 +365,6 @@
     length = documents.shape[0]
     position = jnp.arange(length, dtype=jnp.int32)
     return (position[None, :] <= position[:, None]) & (documents[:, None] == documents[None, :])
-
-
-def project(normed, weight):
-    return jnp.dot(normed, weight, preferred_element_type=jnp.float32).astype(jnp.bfloat16)
 
 
 def contract_last(left_side, right_side):
@@ -83,37 +417,23 @@
     return from_behind(payload, "pp", offset)
 
 
-def per_copy(left_side, right_side, copies):
-    length = left_side.shape[0] // copies
-    product = jnp.einsum(
-        "nsd,nse->nde",
-        left_side.reshape(copies, length, left_side.shape[1]),
-        right_side.reshape(copies, length, right_side.shape[1]),
-        preferred_element_type=jnp.float32,
-    )
-    kept = lax.optimization_barrier(product.astype(jnp.bfloat16))
-    return jnp.sum(kept.astype(jnp.float32), axis=0)
-
-
 def body(act_in, stash_in, grad_in, doc_ids, query_weight, key_weight, value_weight, out_weight):
     kv_local = key_weight.shape[2] // HEAD
     forward_rows = act_in[0, 0]
     backward_rows = stash_in[0, 0]
     grad_rows = grad_in[0, 0]
-    normed_ahead, unused_inverse = norm_rows(forward_rows)
-    normed_back, inverse_back = norm_rows(backward_rows)
-    ahead_full, back_full, grad_full = (
-        lax.all_gather(normed_ahead, "tp", axis=0, tiled=True),
-        lax.all_gather(normed_back, "tp", axis=0, tiled=True),
-        lax.all_gather(grad_rows, "tp", axis=0, tiled=True),
-    )
     w_query = query_weight[0]
     w_key = key_weight[0]
     w_value = value_weight[0]
     w_out = out_weight[0]
-    queries_ahead = project(ahead_full, w_query)
-    keys_ahead = project(ahead_full, w_key)
-    values_ahead = project(ahead_full, w_value)
+    n, copies = lax.axis_size("tp"), lax.axis_size("dp")
+    (
+        queries_back, keys_back, values_back, queries_ahead, keys_ahead, values_ahead,
+        dmixed, normed_cols,
+    ) = gather_call(
+        n, copies, forward_rows, grad_rows, backward_rows, w_query, w_key, w_value, w_out
+    )
+    unused_normed, inverse_back = norm_rows(backward_rows)
     query_heads, key_heads, value_heads = split_heads(
         queries_ahead, keys_ahead, values_ahead, kv_local
     )
@@ -123,14 +443,10 @@
     )
     mixed_ahead = mixed_ahead.astype(jnp.bfloat16).reshape(queries_ahead.shape)
     forward_sum = contract_last(mixed_ahead, w_out)
-    queries_back = project(back_full, w_query)
-    keys_back = project(back_full, w_key)
-    values_back = project(back_full, w_value)
     query_back_heads, key_back_heads, unused_values = split_heads(
         queries_back, keys_back, values_back, kv_local
     )
     probs_back = attend_probs(query_back_heads, key_back_heads, allowed(doc_ids[0, 0, 1]))
-    dmixed = jnp.dot(grad_full, w_out, preferred_element_type=jnp.float32).astype(jnp.bfloat16)
     dqueries, dkeys, dvalues = attend_back(
         dmixed, queries_back, keys_back, values_back, probs_back, kv_local
     )
@@ -141,13 +457,9 @@
         + contract_last(dkey_cols, w_key)
         + contract_last(dvalue_cols, w_value)
     )
-    forward_share, backward_share = (
-        lax.psum_scatter(
-            forward_sum.astype(jnp.bfloat16), "tp", scatter_dimension=0, tiled=True
-        ).astype(jnp.float32),
-        lax.psum_scatter(
-            dnormed.astype(jnp.bfloat16), "tp", scatter_dimension=0, tiled=True
-        ).astype(jnp.float32),
+    forward_share, backward_share, all_queries, all_keys, all_values = scatter_call(
+        n, copies, forward_sum.astype(jnp.bfloat16), dnormed.astype(jnp.bfloat16),
+        dqueries, dkey_cols, dvalue_cols,
     )
     outgoing = (forward_rows.astype(jnp.float32) + forward_share).astype(jnp.bfloat16)
     scaled = backward_rows.astype(jnp.float32) * inverse_back
@@ -158,16 +470,9 @@
     ).astype(jnp.bfloat16)
     act_out = handoff(outgoing, 1)[None, None]
     grad_out = handoff(grad_back, -1)[None, None]
-    copies = lax.axis_size("dp")
-    normed_cols = lax.all_to_all(back_full, "dp", split_axis=1, concat_axis=0, tiled=True)
-    all_queries, all_keys, all_values = (
-        lax.all_gather(dqueries, "dp", axis=0, tiled=True),
-        lax.all_gather(dkey_cols, "dp", axis=0, tiled=True),
-        lax.all_gather(dvalue_cols, "dp", axis=0, tiled=True),
-    )
-    grad_query = per_copy(normed_cols, all_queries, copies)[None]
-    grad_key = per_copy(normed_cols, all_keys, copies)[None]
-    grad_value = per_copy(normed_cols, all_values, copies)[None]
+    grad_query, grad_key, grad_value = (
+        grad[None] for grad in weights_call(normed_cols, all_queries, all_keys, all_values)
+    )
     return (act_out, grad_out, grad_query, grad_key, grad_value)
 
 

time: 209 us -> 144 us (0.69)
  Pallas kernels: 0 us -> 110 us
  waiting for transfers between devices: 55.7 us -> 0.01 us
  matrix products: 62.8 us -> 16.7 us
  blocking collectives: 26.5 us -> 0 us
  other arithmetic: 27.1 us -> 1.78 us
  between operations: 14 us -> 0.96 us
  local copies, waits for them, and re-layouts: 11.4 us -> 5.99 us
    pallas_call x0 -> x3, Pallas kernels: none -> 110 us  [the longest x1 61.7 us: gather_call(): pl.pallas_call(functools.partial(gather_kernel, n, copies), out_shape=[ja...]
    all_gather x3 -> x0, waiting for transfers between devices: 45.7 us -> none  [the longest x1 25.2 us: body(): lax.all_gather(normed_back, 'tp', axis=0, tiled=True)]
    dot_general x10 -> x0, matrix products: 33.1 us -> none  [the longest x6 16.7 us: project(): jnp.dot(normed, weight, preferred_element_type=jnp.float32)]
    all_gather x3 -> x0, blocking collectives: 26.5 us -> none  [the longest x1 13.3 us: body(): lax.all_gather(dkey_cols, 'dp', axis=0, tiled=True)]
    reduce_sum x3 -> x0, other arithmetic: 15.2 us -> none  [per_copy(): return jnp.sum(kept.astype(jnp.float32), axis=0)]
    reduce_scatter x2 -> x0, waiting for transfers between devices: 9.31 us -> none  [the longest x1 9.31 us: body(): lax.psum_scatter(forward_sum.astype(jnp.bfloat16), 'tp', scatter_dimensio...]
    all_to_all x1 -> x0, starting transfers between devices: 3.58 us -> none  [body(): lax.all_to_all(back_full, 'dp', split_axis=1, concat_axis=0, tiled=True)]
    all_gather x3 -> x0, local copies, waits for them, and re-layouts: 3.56 us -> none  [the longest x1 2.04 us: body(): lax.all_gather(dqueries, 'dp', axis=0, tiled=True)]
  transfers between devices with their start and end apart: 8 -> 2, of which waited for: 3 -> 0; matrix products, arithmetic and copies ran while one was open for 46% -> 0% of each run, Pallas kernels for 0% -> 5%
where the time goes in v1:
time: 144 us; the launch traced here: 143 us
  Pallas kernels  110 us (76%)
  matrix products  16.7 us (12%)
  starting transfers between devices  8.48 us (6%)
  local copies, waits for them, and re-layouts  5.99 us (4%)
  other arithmetic  1.78 us (1%)
    pallas_call x1, Pallas kernels, gather_call(): pl.pallas_call(functools.partial(gather_kernel, n, copies), out_shape=[ja...  61.7 us
    pallas_call x1, Pallas kernels, scatter_call(): pl.pallas_call(functools.partial(scatter_kernel, n, copies), out_shape=[j...  40.6 us
    dot_general x4, matrix products, contract_last(): lax.dot_general(left_side, right_side, (((1,), (1,)), ((), ())), preferre...  14.4 us
    ppermute x2, starting transfers between devices, from_behind(): return lax.ppermute(value, axis, pairs)  8.48 us
    pallas_call x1, Pallas kernels, weights_call(): pl.pallas_call(functools.partial(weights_kernel, copies), grid=(piece //...  7.29 us
  transfers between devices with their start and end apart: 2, of which 0 were waited for; matrix products, arithmetic and copies ran while one was open for 0% of the time, Pallas kernels for 5%

profile of v1, /device:TPU:1, one launch (start us, length us, event | category | flops | bytes accessed | tf_op | source)
XLA Modules:
  0.0 143.5 jit_solution(1329474443908314995)
XLA Ops:
  0.6 1.1 fusion.33
  1.7 0.8 slice_bitcast_fusion
  2.5 61.7 %shard_map.119 = (bf16[128,1024]{1,0:T(8,128)(2,1)}, bf16[128,256]{1,0:T(8,128)(2,1)}, bf16[128,256]{1,0:T(8,128)(2,1)}, bf16[128,1024]{1,0:T(8,128)(2,1)}, bf16...) custom-call(bf16[32,4096]{1,0:T(8,128)(2,1)} %bitcast.99, ...), custom_call_target="tpu_custom_call" | custom-call | flops 40000000000 | bytes 30000000 | tf_op jit(solution)/shard_map/pallas_call | solution.py:194
  64.2 0.9 reshape.67
  65.1 1.1 reshape.68
  66.4 0.3 fusion.60
  66.7 0.2 fusion.14
  67.7 0.4 fusion.65
  68.2 0.3 fusion.16
  68.5 0.3 convolution_convert_fusion.1
  68.8 0.2 fusion.17
  69.2 6.3 %fusion.54 = f32[128,4096]{1,0:T(8,128)S(1)} fusion(bf16[128,1024]{0,1:T(8,128)(2,1)S(1)} %bitcast.103, bf16[1,4096,1024]{2,1,0:T(8,128)(2,1)} %param.12), kind=kOutput, calls=%fused_computation.67 | convolution fusion | flops 1073741824 | bytes 10747904 | tf_op jit(solution)/shard_map/dot_general | solution.py:371
  75.9 0.3 convolution_convert_fusion.2
  76.3 6.4 %convolution_convert_fusion.fsum = bf16[128,4096]{1,0:T(8,128)(2,1)S(1)} fusion(bf16[128,1024]{0,1:T(8,128)(2,1)S(1)} %bitcast.108, bf16[1,4096,1024]{2,1,0:T(8,128)(2,1)} %param.15), kind=kOutput, calls=%fused_computation.6 | convolution fusion | flops 1074266112 | bytes 9699328 | tf_op jit(solution)/shard_map/dot_general | solution.py:371
  82.7 0.8 convolution_add_fusion.1
  83.5 0.8 copy-done.3
  84.3 0.8 fusion.3.bsum
  85.1 40.6 %shard_map.120 = (f32[32,4096]{1,0:T(8,128)S(1)}, f32[32,4096]{1,0:T(8,128)S(1)}, bf16[2,128,1024]{2,1,0:T(8,128)(2,1)S(1)}, bf16[2,128,256]{2,1,0:T(8,128)(2,1)S(1)}, bf16[2,128,256]{2,1,0:T(8,128)(2,1)S(1)}) custom-call(bf16[128,4096]{1,0:T(8,128)(2,1)S(1)} %convolution_convert_fusion.fsum, bf16[128,4096]{1,0:T(8,128)(2,1)S(1)} %fusion.3.bsum, ...), custom_call_target="tpu_custom_call" | custom-call | flops 30000001024 | bytes 10000000 | tf_op jit(solution)/shard_map/pallas_call | solution.py:305
  125.8 0.3 fusion.28
  126.2 6.9 %collective-permute-start.1 = (bf16[32,4096]{1,0:T(8,128)(2,1)S(1)}, bf16[32,4096]{1,0:T(8,128)(2,1)S(1)}, u32[]{:S(2)}, u32[]{:S(2)}) collective-permute-start(bf16[32,4096]{1,0:T(8,128)(2,1)S(1)} %fusion.32), channel_id=1, source_target_pairs={{0,24},{8,0},{16,8},{24,16},{1,25},{9,1},{17,9},{25,17},{2,26},{10... | collective-permute-start | bytes 786440 | tf_op jit(solution)/shard_map/ppermute | solution.py:20
  133.2 1.5 %collective-permute-start = (bf16[32,4096]{1,0:T(8,128)(2,1)S(1)}, bf16[32,4096]{1,0:T(8,128)(2,1)S(1)}, u32[]{:S(2)}, u32[]{:S(2)}) collective-permute-start(bf16[32,4096]{1,0:T(8,128)(2,1)S(1)} %add_convert_fusion), channel_id=1, source_target_pairs={{0,8},{8,16},{16,24},{24,0},{1,9},{9,17},{17,25},{25,1},{2,10},{10... | collective-permute-start | bytes 786440 | tf_op jit(solution)/shard_map/ppermute | solution.py:20
  134.8 7.3 %shard_map.121 = (f32[2048,1024]{1,0:T(8,128)}, f32[2048,256]{1,0:T(8,128)}, f32[2048,256]{1,0:T(8,128)}) custom-call(bf16[2,128,2048]{2,1,0:T(8,128)(2,1)S(1)} %copy-done, bf16[2,128,1024]{2,1,0:T(8,128)(2,1)S(1)} %get-tuple-element.31.aq, bf16[2,128,256]{2,1,0:T(8,128)(2,1)S(1)} %get-tuple-element.32.ak, bf16[2,128,256]{2,1,0:T(8,128)(2,1)S(1)} %get-tuple-element.33.av), custom_call_target="tpu_custom_call" | custom-call | flops 1610612736 | bytes 12582912 | tf_op jit(solution)/shard_map/pallas_call | solution.py:343
  142.1 0.7 copy.71
  142.8 0.7 copy.72
  (39 shorter events, 1.7 us)
Async XLA Ops:
  64.2 2.8 %copy-start.10 = (bf16[128,256]{1,0:T(8,128)(2,1)S(1)}, bf16[128,256]{1,0:T(8,128)(2,1)}, u32[]{:S(2)}) copy-start(bf16[128,256]{1,0:T(8,128)(2,1)} %get-tuple-element.24) | copy-start | bytes 196612
  64.2 2.9 %copy-start.9 = (bf16[128,256]{1,0:T(8,128)(2,1)S(1)}, bf16[128,256]{1,0:T(8,128)(2,1)}, u32[]{:S(2)}) copy-start(bf16[128,256]{1,0:T(8,128)(2,1)} %get-tuple-element.26) | copy-start | bytes 196612
  64.2 3.0 %copy-start.5 = (bf16[128,1024]{1,0:T(8,128)(2,1)S(1)}, bf16[128,1024]{1,0:T(8,128)(2,1)}, u32[]{:S(2)}) copy-start(bf16[128,1024]{1,0:T(8,128)(2,1)} %get-tuple-element.25) | copy-start | bytes 786436
  64.2 3.1 %copy-start.4 = (bf16[128,1024]{1,0:T(8,128)(2,1)S(1)}, bf16[128,1024]{1,0:T(8,128)(2,1)}, u32[]{:S(2)}) copy-start(bf16[128,1024]{1,0:T(8,128)(2,1)} %get-tuple-element.27) | copy-start | bytes 786436
  69.2 6.4 %copy-start.8 = (bf16[128,256]{1,0:T(8,128)(2,1)S(1)}, bf16[128,256]{1,0:T(8,128)(2,1)}, u32[]{:S(2)}) copy-start(bf16[128,256]{1,0:T(8,128)(2,1)} %get-tuple-element.21) | copy-start | bytes 196612
  76.2 6.5 %copy-start.2 = (bf16[1,4096,256]{2,1,0:T(8,128)(2,1)S(1)}, bf16[1,4096,256]{2,1,0:T(8,128)(2,1)}, u32[]{:S(2)}) copy-start(bf16[1,4096,256]{2,1,0:T(8,128)(2,1)} %param.13) | copy-start | bytes 6291460
  82.7 1.6 %copy-start.3 = (bf16[1,4096,256]{2,1,0:T(8,128)(2,1)S(1)}, bf16[1,4096,256]{2,1,0:T(8,128)(2,1)}, u32[]{:S(2)}) copy-start(bf16[1,4096,256]{2,1,0:T(8,128)(2,1)} %param.14) | copy-start | bytes 6291460
  85.1 40.6 %copy-start.1 = (bf16[1,1,32,4096]{3,2,1,0:T(8,128)(2,1)S(1)}, bf16[1,1,32,4096]{3,2,1,0:T(8,128)(2,1)}, u32[]{:S(2)}) copy-start(bf16[1,1,32,4096]{3,2,1,0:T(8,128)(2,1)} %param.9) | copy-start | bytes 786436
  85.1 40.9 %copy-start.6 = (bf16[1,1,32,4096]{3,2,1,0:T(8,128)(2,1)S(1)}, bf16[1,1,32,4096]{3,2,1,0:T(8,128)(2,1)}, u32[]{:S(2)}) copy-start(bf16[1,1,32,4096]{3,2,1,0:T(8,128)(2,1)} %param.10) | copy-start | bytes 786436
  125.7 7.4 %copy-start.7 = (bf16[1,1,32,4096]{3,2,1,0:T(8,128)(2,1)S(1)}, bf16[1,1,32,4096]{3,2,1,0:T(8,128)(2,1)}, u32[]{:S(2)}) copy-start(bf16[1,1,32,4096]{3,2,1,0:T(8,128)(2,1)} %param.8) | copy-start | bytes 786436
  125.8 9.0 %copy-start = (bf16[2,128,2048]{2,1,0:T(8,128)(2,1)S(1)}, bf16[2,128,2048]{2,1,0:T(8,128)(2,1)}, u32[]{:S(2)}) copy-start(bf16[2,128,2048]{2,1,0:T(8,128)(2,1)} %get-tuple-element.30.ncols) | copy-start | bytes 3145732
  126.2 15.8 %collective-permute-start.1 = (bf16[32,4096]{1,0:T(8,128)(2,1)S(1)}, bf16[32,4096]{1,0:T(8,128)(2,1)S(1)}, u32[]{:S(2)}, u32[]{:S(2)}) collective-permute-start(bf16[32,4096]{1,0:T(8,128)(2,1)S(1)} %fusion.32), channel_id=1, source_target_pairs={{0,24},{8,0},{16,8},{24,16},{1,25},{9,1},{17,9},{25,17},{2,26},{10... | collective-permute-start | bytes 786440 | tf_op jit(solution)/shard_map/ppermute | solution.py:20
  133.2 8.8 %collective-permute-start = (bf16[32,4096]{1,0:T(8,128)(2,1)S(1)}, bf16[32,4096]{1,0:T(8,128)(2,1)S(1)}, u32[]{:S(2)}, u32[]{:S(2)}) collective-permute-start(bf16[32,4096]{1,0:T(8,128)(2,1)S(1)} %add_convert_fusion), channel_id=1, source_target_pairs={{0,8},{8,16},{16,24},{24,0},{1,9},{9,17},{17,25},{25,1},{2,10},{10... | collective-permute-start | bytes 786440 | tf_op jit(solution)/shard_map/ppermute | solution.py:20

commit v2 on v1

--- a/solution.py
+++ b/solution.py
@@ -54,11 +54,78 @@
     pl.semaphore_wait(barrier, ends + copies - 1)
 
 
+class LineSum:
+    def __init__(self, n, me, rows, whole, slots, ss, rs):
+        self.n, self.me, self.rows, self.whole = n, me, rows, whole
+        self.slots, self.ss, self.rs = slots, ss, rs
+
+    def routes(self, k):
+        return ((0, self.n - 1 - k), (1, k))
+
+    def every(self):
+        return [route for k in range(self.n - 1) for route in self.routes(k)]
+
+    def copy(self, side, dest, first):
+        part = self.whole.at[pl.ds(dest * self.rows, self.rows), :]
+        slot = self.slots.at[side, dest]
+        return remote(
+            part if first else slot, slot, self.ss.at[side, dest], self.rs.at[side, dest],
+            "tp", self.me + (1 if side == 0 else -1),
+        )
+
+    def landed(self, side, dest):
+        slot = self.slots.at[side, dest]
+        remote(
+            slot, slot, self.ss.at[side, dest], self.rs.at[side, dest], "tp",
+            jnp.where(self.me == 0, 1, self.me - 1),
+        ).wait_recv()
+
+    def roles(self, side, dest):
+        me, n = self.me, self.n
+        if side == 0:
+            return me == 0, (me > 0) & (me < dest)
+        return me == n - 1, (me < n - 1) & (me > dest)
+
+    def begin(self):
+        for side, dest in self.every():
+            @pl.when(self.roles(side, dest)[0])
+            def _():
+                self.copy(side, dest, True).start()
+
+    def middle(self, k):
+        slots, rows = self.slots, self.rows
+        for side, dest in self.routes(k):
+            @pl.when(self.roles(side, dest)[1])
+            def _():
+                self.landed(side, dest)
+                slots[side, dest] = (
+                    slots[side, dest].astype(jnp.float32)
+                    + self.whole[dest * rows : (dest + 1) * rows, :].astype(jnp.float32)
+                ).astype(jnp.bfloat16)
+                self.copy(side, dest, False).start()
+
+    def finish(self, out):
+        me, rows = self.me, self.rows
+        out[...] = self.whole[pl.ds(pl.multiple_of(me * rows, rows), rows), :].astype(jnp.float32)
+        for side, dest in self.every():
+            @pl.when(me == dest)
+            def _():
+                self.landed(side, dest)
+                out[...] += self.slots[side, dest].astype(jnp.float32)
+        for side, dest in self.every():
+            first, middle = self.roles(side, dest)
+
+            @pl.when(first | middle)
+            def _():
+                self.copy(side, dest, False).wait_send()
+
+
 def gather_kernel(
     n, copies,
-    act, stash, grad, wq, wk, wv, wo,
-    qb, kb, vb, qf, kf, vf, dm, ncols,
-    full, normed, vq, vk, vv, vo, wsem, ss, rs, dss, drs,
+    act, stash, grad, mask, wq, wk, wv, wo,
+    qb, kb, vb, dm, ncols, fshare,
+    full, normed, vq, vk, vv, vo, qf, kf, vf, mixed, fsum, slots,
+    wsem, ss, rs, dss, drs, rss, rrs,
 ):
     me = lax.axis_index("tp")
     mine = lax.axis_index("dp")
@@ -138,6 +205,30 @@
             inverse = lax.rsqrt(jnp.mean(wide * wide, axis=-1, keepdims=True) + epsilon)
             normed[where, :] = (wide * inverse).astype(jnp.bfloat16)
 
+    def attend():
+        heads = qf.shape[1] // HEAD
+        group_size = qf.shape[1] // kf.shape[1]
+        for h in range(heads):
+            columns = slice(h * HEAD, (h + 1) * HEAD)
+            k = h // group_size
+            kv_columns = slice(k * HEAD, (k + 1) * HEAD)
+            scores = contract_last(qf[:, columns], kf[:, kv_columns]) * (1.0 / math.sqrt(HEAD))
+            scores = jnp.where(mask[...] > 0.5, scores, -jnp.inf)
+            weights = jnp.exp(scores - jnp.max(scores, axis=-1, keepdims=True))
+            probs = (weights / jnp.sum(weights, axis=-1, keepdims=True)).astype(jnp.bfloat16)
+            mixed[:, columns] = jnp.dot(
+                probs, vf[:, kv_columns], preferred_element_type=jnp.float32
+            ).astype(jnp.bfloat16)
+
+    def project_out():
+        tile = 256
+
+        @pl.loop(0, width // tile)
+        def _(t):
+            features = pl.ds(pl.multiple_of(t * tile, tile), tile)
+            fsum[:, features] = contract_last(mixed[...], vo[features, :]).astype(jnp.bfloat16)
+
+    line = LineSum(n, me, rows, fsum, slots, rss, rrs)
     start(0, 1)
     start(1, 1)
     for a in range(3):
@@ -149,9 +240,17 @@
     normalise(0)
     for load in loads:
         load.wait()
+    multiply(normed, vq, qf)
+    multiply(normed, vk, kf)
+    multiply(normed, vv, vf)
+    for step in range(2, n):
+        arrive(1, step)
+    attend()
+    arrive(2, 1)
+    project_out()
+    line.begin()
+    normalise(1)
     multiply(normed, vq, qb)
-    multiply(normed, vk, kb)
-    multiply(normed, vv, vb)
     trades = []
     for offset in range(1, copies):
         other = lax.rem(mine + offset, copies)
@@ -162,18 +261,19 @@
         trade.start()
         trades.append(trade)
     ncols[mine] = normed[:, pl.ds(pl.multiple_of(mine * piece, piece), piece)]
-    for step in range(2, n):
-        arrive(1, step)
-    arrive(2, 1)
-    multiply(full.at[1], vo, dm)
-    for step in range(2, n):
+    arrive(2, 2) if n > 2 else None
+    line.middle(0)
+    multiply(normed, vk, kb)
+    multiply(normed, vv, vb)
+    for step in range(3, n):
         arrive(2, step)
+        line.middle(step - 2)
+    if n > 2:
+        line.middle(n - 2)
+    multiply(full.at[2], vo, dm)
+    line.finish(fshare)
     for trade in trades:
         trade.wait()
-    normalise(2)
-    multiply(normed, vq, qf)
-    multiply(normed, vk, kf)
-    multiply(normed, vv, vf)
     for a in range(3):
         for step in range(1, n):
             for side in range(2):
@@ -182,42 +282,47 @@
                     hop(a, side, step).wait_send()
 
 
-def gather_call(n, copies, act, grad, stash, wq, wk, wv, wo):
+def gather_call(n, copies, act, grad, stash, mask, wq, wk, wv, wo):
     rows, width = act.shape
     seq = rows * n
     bf = jnp.bfloat16
     vmem = pl.BlockSpec(memory_space=pltpu.VMEM)
     anywhere = pl.BlockSpec(memory_space=pl.ANY)
-    shapes = [(seq, w.shape[1]) for w in (wq, wk, wv)] * 2 + [(seq, wo.shape[1])]
+    heads = [(seq, w.shape[1]) for w in (wq, wk, wv)]
+    shapes = heads + [(seq, wo.shape[1])]
     shapes += [(copies, seq, width // copies)]
     sem = pltpu.SemaphoreType.DMA
     return pl.pallas_call(
         functools.partial(gather_kernel, n, copies),
-        out_shape=[jax.ShapeDtypeStruct(shape, bf) for shape in shapes],
-        in_specs=[vmem] * 3 + [anywhere] * 4,
-        out_specs=[vmem] * len(shapes),
+        out_shape=[jax.ShapeDtypeStruct(shape, bf) for shape in shapes]
+        + [jax.ShapeDtypeStruct((rows, width), jnp.float32)],
+        in_specs=[vmem] * 4 + [anywhere] * 4,
+        out_specs=[vmem] * (len(shapes) + 1),
         scratch_shapes=[pltpu.VMEM((3, seq, width), bf), pltpu.VMEM((seq, width), bf)]
         + [pltpu.VMEM(w.shape, bf) for w in (wq, wk, wv, wo)]
-        + [sem((4,)), sem((3, 2, n)), sem((3, 2, n)), sem((copies,)), sem((copies,))],
+        + [pltpu.VMEM(shape, bf) for shape in heads]
+        + [pltpu.VMEM((seq, wo.shape[1]), bf), pltpu.VMEM((seq, width), bf)]
+        + [pltpu.VMEM((2, n, rows, width), bf)]
+        + [sem((4,)), sem((3, 2, n)), sem((3, 2, n)), sem((copies,)), sem((copies,))]
+        + [sem((2, n)), sem((2, n))],
         compiler_params=pltpu.CompilerParams(
             collective_id=0, has_side_effects=True, vmem_limit_bytes=VMEM_LIMIT
         ),
         cost_estimate=pl.CostEstimate(
             flops=40_000_000_000, bytes_accessed=30_000_000, transcendentals=0
         ),
-    )(stash, grad, act, wq, wk, wv, wo)
+    )(act, stash, grad, mask, wq, wk, wv, wo)
 
 
 def scatter_kernel(
     n, copies,
-    fsum, bsum, dq, dk, dv,
-    fshare, bshare, aq, ak, av,
+    bsum, dq, dk, dv,
+    bshare, aq, ak, av,
     slots, ss, rs, dss, drs,
 ):
     me = lax.axis_index("tp")
     mine = lax.axis_index("dp")
-    rows, width = fshare.shape
-    sums = (bsum, fsum)
+    rows = bshare.shape[0]
     greet(n, copies, me, mine)
     trades = []
     for offset in range(1, copies):
@@ -229,88 +334,32 @@
             trade.start()
             trades.append(trade)
 
-    def copy(a, side, dest, first):
-        toward = 1 if side == 0 else -1
-        part = sums[a].at[pl.ds(dest * rows, rows), :]
-        return remote(
-            part if first else slots.at[a, side, dest], slots.at[a, side, dest],
-            ss.at[a, side, dest], rs.at[a, side, dest], "tp", me + toward,
-        )
-
-    def landed(a, side, dest):
-        slot = slots.at[a, side, dest]
-        remote(
-            slot, slot, ss.at[a, side, dest], rs.at[a, side, dest], "tp",
-            jnp.where(me == 0, 1, me - 1),
-        ).wait_recv()
-
-    def roles(side, dest):
-        if side == 0:
-            return me == 0, (me > 0) & (me < dest)
-        return me == n - 1, (me < n - 1) & (me > dest)
-
-    routes = []
-    for k in range(n - 1):
-        for side in range(2):
-            routes.append((side, n - 1 - k if side == 0 else k))
-    for a in range(2):
-        for side, dest in routes:
-            first, middle = roles(side, dest)
-
-            @pl.when(first)
-            def _():
-                copy(a, side, dest, True).start()
-
+    line = LineSum(n, me, rows, bsum, slots, ss, rs)
+    line.begin()
     aq[mine] = dq[...]
     ak[mine] = dk[...]
     av[mine] = dv[...]
-    for a in range(2):
-        for side, dest in routes:
-            first, middle = roles(side, dest)
-
-            @pl.when(middle)
-            def _():
-                landed(a, side, dest)
-                slots[a, side, dest] = (
-                    slots[a, side, dest].astype(jnp.float32)
-                    + sums[a][dest * rows : (dest + 1) * rows, :].astype(jnp.float32)
-                ).astype(jnp.bfloat16)
-                copy(a, side, dest, False).start()
-
-    for a, out in enumerate((bshare, fshare)):
-        out[...] = sums[a][pl.ds(pl.multiple_of(me * rows, rows), rows), :].astype(jnp.float32)
-        for side, dest in routes:
-            @pl.when(me == dest)
-            def _():
-                landed(a, side, dest)
-                out[...] += slots[a, side, dest].astype(jnp.float32)
-
-    for a in range(2):
-        for side, dest in routes:
-            first, middle = roles(side, dest)
-
-            @pl.when(first | middle)
-            def _():
-                copy(a, side, dest, False).wait_send()
-
+    for k in range(n - 1):
+        line.middle(k)
+    line.finish(bshare)
     for trade in trades:
         trade.wait()
 
 
-def scatter_call(n, copies, fsum, bsum, dq, dk, dv):
-    seq, width = fsum.shape
+def scatter_call(n, copies, bsum, dq, dk, dv):
+    seq, width = bsum.shape
     rows = seq // n
     vmem = pl.BlockSpec(memory_space=pltpu.VMEM)
     sem = pltpu.SemaphoreType.DMA
     return pl.pallas_call(
         functools.partial(scatter_kernel, n, copies),
-        out_shape=[jax.ShapeDtypeStruct((rows, width), jnp.float32)] * 2
+        out_shape=[jax.ShapeDtypeStruct((rows, width), jnp.float32)]
         + [jax.ShapeDtypeStruct((copies,) + g.shape, jnp.bfloat16) for g in (dq, dk, dv)],
-        in_specs=[vmem] * 5,
-        out_specs=[vmem] * 5,
+        in_specs=[vmem] * 4,
+        out_specs=[vmem] * 4,
         scratch_shapes=[
-            pltpu.VMEM((2, 2, n, rows, width), jnp.bfloat16),
-            sem((2, 2, n)), sem((2, 2, n)), sem((copies, 3)), sem((copies, 3)),
+            pltpu.VMEM((2, n, rows, width), jnp.bfloat16),
+            sem((2, n)), sem((2, n)), sem((copies, 3)), sem((copies, 3)),
         ],
         compiler_params=pltpu.CompilerParams(
             collective_id=1, has_side_effects=True, vmem_limit_bytes=40 * 1024 * 1024
@@ -318,7 +367,7 @@
         cost_estimate=pl.CostEstimate(
             flops=30_000_000_000, bytes_accessed=10_000_000, transcendentals=0
         ),
-    )(fsum, bsum, dq, dk, dv)
+    )(bsum, dq, dk, dv)
 
 
 def weights_kernel(copies, ncols, aq, ak, av, gq, gk, gv):
@@ -427,22 +476,11 @@
     w_value = value_weight[0]
     w_out = out_weight[0]
     n, copies = lax.axis_size("tp"), lax.axis_size("dp")
-    (
-        queries_back, keys_back, values_back, queries_ahead, keys_ahead, values_ahead,
-        dmixed, normed_cols,
-    ) = gather_call(
-        n, copies, forward_rows, grad_rows, backward_rows, w_query, w_key, w_value, w_out
+    queries_back, keys_back, values_back, dmixed, normed_cols, forward_share = gather_call(
+        n, copies, forward_rows, grad_rows, backward_rows,
+        allowed(doc_ids[0, 0, 0]).astype(jnp.float32), w_query, w_key, w_value, w_out,
     )
     unused_normed, inverse_back = norm_rows(backward_rows)
-    query_heads, key_heads, value_heads = split_heads(
-        queries_ahead, keys_ahead, values_ahead, kv_local
-    )
-    probs_ahead = attend_probs(query_heads, key_heads, allowed(doc_ids[0, 0, 0]))
-    mixed_ahead = jnp.einsum(
-        "hgij,jhd->ihgd", probs_ahead, value_heads, preferred_element_type=jnp.float32
-    )
-    mixed_ahead = mixed_ahead.astype(jnp.bfloat16).reshape(queries_ahead.shape)
-    forward_sum = contract_last(mixed_ahead, w_out)
     query_back_heads, key_back_heads, unused_values = split_heads(
         queries_back, keys_back, values_back, kv_local
     )
@@ -457,9 +495,8 @@
         + contract_last(dkey_cols, w_key)
         + contract_last(dvalue_cols, w_value)
     )
-    forward_share, backward_share, all_queries, all_keys, all_values = scatter_call(
-        n, copies, forward_sum.astype(jnp.bfloat16), dnormed.astype(jnp.bfloat16),
-        dqueries, dkey_cols, dvalue_cols,
+    backward_share, all_queries, all_keys, all_values = scatter_call(
+        n, copies, dnormed.astype(jnp.bfloat16), dqueries, dkey_cols, dvalue_cols
     )
     outgoing = (forward_rows.astype(jnp.float32) + forward_share).astype(jnp.bfloat16)
     scaled = backward_rows.astype(jnp.float32) * inverse_back

time: 144 us -> 145 us (level)
  matrix products: 16.7 us -> 11.1 us
  starting transfers between devices: 8.48 us -> 11.2 us
  Pallas kernels: 110 us -> 112 us
    pallas_call x1, Pallas kernels: 61.7 us -> 73.5 us  [gather_call(): pl.pallas_call(functools.partial(gather_kernel, n, copies), out_shape=[ja...]
    pallas_call x1, Pallas kernels: 40.6 us -> 31.2 us  [scatter_call(): pl.pallas_call(functools.partial(scatter_kernel, n, copies), out_shape=[j...]
    dot_general x4 -> x3, matrix products: 14.4 us -> 9.7 us  [contract_last(): lax.dot_general(left_side, right_side, (((1,), (1,)), ((), ())), preferre...]
    ppermute x2, starting transfers between devices: 8.48 us -> 11.2 us  [from_behind(): return lax.ppermute(value, axis, pairs)]
  transfers between devices with their start and end apart: 2 -> 2, of which waited for: 0 -> 0; matrix products, arithmetic and copies ran while one was open for 0% -> 11% of each run, Pallas kernels for 5% -> 27%
where the time goes in v2:
time: 145 us; the launch traced here: 144 us
  Pallas kernels  112 us (77%)
  starting transfers between devices  11.2 us (8%)
  matrix products  11.1 us (8%)
  local copies, waits for them, and re-layouts  5.81 us (4%)
  other arithmetic  2.55 us (2%)
    pallas_call x1, Pallas kernels, gather_call(): pl.pallas_call(functools.partial(gather_kernel, n, copies), out_shape=[ja...  73.5 us
    pallas_call x1, Pallas kernels, scatter_call(): pl.pallas_call(functools.partial(scatter_kernel, n, copies), out_shape=[j...  31.2 us
    ppermute x2, starting transfers between devices, from_behind(): return lax.ppermute(value, axis, pairs)  11.2 us
    dot_general x3, matrix products, contract_last(): lax.dot_general(left_side, right_side, (((1,), (1,)), ((), ())), preferre...  9.7 us
    pallas_call x1, Pallas kernels, weights_call(): pl.pallas_call(functools.partial(weights_kernel, copies), grid=(piece //...  7.29 us
  transfers between devices with their start and end apart: 2, of which 0 were waited for; matrix products, arithmetic and copies ran while one was open for 11% of the time, Pallas kernels for 27%

profile of v2, /device:TPU:1, one launch (start us, length us, event | category | flops | bytes accessed | tf_op | source)
XLA Modules:
  0.0 143.5 jit_solution(6428908358981838619)
XLA Ops:
  0.6 0.8 slice_bitcast_fusion
  1.4 0.7 fusion.32
  2.1 73.5 %shard_map.119 = (bf16[128,1024]{1,0:T(8,128)(2,1)}, bf16[128,256]{1,0:T(8,128)(2,1)}, bf16[128,256]{1,0:T(8,128)(2,1)}, bf16[128,1024]{1,0:T(8,128)(2,1)}, bf16...) custom-call(bf16[32,4096]{1,0:T(8,128)(2,1)} %bitcast.90, bf16[32,4096]{1,0:T(8,128)(2,1)} %bitcast.76, ...), custom_call_target="tpu_custom_call" | custom-call | flops 40000000000 | bytes 30000000 | tf_op jit(solution)/shard_map/pallas_call | solution.py:295
  75.6 1.1 add_convert_fusion
  76.8 10.4 %collective-permute-start = (bf16[32,4096]{1,0:T(8,128)(2,1)S(1)}, bf16[32,4096]{1,0:T(8,128)(2,1)S(1)}, u32[]{:S(2)}, u32[]{:S(2)}) collective-permute-start(bf16[32,4096]{1,0:T(8,128)(2,1)S(1)} %add_convert_fusion), channel_id=1, source_target_pairs={{0,8},{8,16},{16,24},{24,0},{1,9},{9,17},{17,25},{25,1},{2,10},{10... | collective-permute-start | bytes 786440 | tf_op jit(solution)/shard_map/ppermute | solution.py:20
  87.1 0.2 fusion.28
  87.4 0.9 reshape.52
  88.4 0.9 reshape.54
  89.3 1.1 copy.44
  90.6 0.2 convolution_bitcast_fusion
  90.8 0.4 fusion.46
  91.3 0.3 fusion.11
  91.6 0.3 convolution_convert_fusion
  91.9 0.2 fusion.12
  92.3 6.3 %fusion.41 = f32[128,4096]{1,0:T(8,128)S(1)} fusion(bf16[128,1024]{0,1:T(8,128)(2,1)S(1)} %bitcast.80, bf16[1,4096,1024]{2,1,0:T(8,128)(2,1)} %param.12), kind=kOutput, calls=%fused_computation.54 | convolution fusion | flops 1073741824 | bytes 10747904 | tf_op jit(solution)/shard_map/dot_general | solution.py:420
  98.9 2.6 %convolution_add_fusion.1 = f32[128,4096]{1,0:T(8,128)S(1)} fusion(f32[128,4096]{1,0:T(8,128)S(1)} %fusion.41, bf16[128,256]{0,1:T(8,128)(2,1)S(1)} %bitcast.84, bf16[1,4096,256]{2,1,0:T(8,128)(2,1)} %param.13), kind=kOutput, calls=%fused_computation.3 | convolution fusion | flops 268959744 | bytes 6356992 | tf_op jit(solution)/shard_map/dot_general | solution.py:420
  101.4 0.8 fusion.2.bsum
  102.3 31.2 %shard_map.120 = (f32[32,4096]{1,0:T(8,128)S(1)}, bf16[2,128,1024]{2,1,0:T(8,128)(2,1)S(1)}, bf16[2,128,256]{2,1,0:T(8,128)(2,1)S(1)}, bf16[2,128,256]{2,1,0:T(8,128)(2,1)S(1)}) custom-call(bf16[128,4096]{1,0:T(8,128)(2,1)S(1)} %fusion.2.bsum, bf16[128,1024]{1,0:T(8,128)(2,1)S(1)} %copy.41.dq, bf16[128,256]{1,0:T(8,128)(2,1)S(1)} %copy.42.dk, ...), custom_call_target="tpu_custom_call" | custom-call | flops 30000001024 | bytes 10000000 | tf_op jit(solution)/shard_map/pallas_call | solution.py:354
  133.5 0.3 fusion.23
  133.8 0.2 fusion.27
  134.0 0.8 collective-permute-start.1
  134.8 7.3 %shard_map.121 = (f32[2048,1024]{1,0:T(8,128)}, f32[2048,256]{1,0:T(8,128)}, f32[2048,256]{1,0:T(8,128)}) custom-call(bf16[2,128,2048]{2,1,0:T(8,128)(2,1)S(1)} %copy-done, bf16[2,128,1024]{2,1,0:T(8,128)(2,1)S(1)} %get-tuple-element.25.aq, bf16[2,128,256]{2,1,0:T(8,128)(2,1)S(1)} %get-tuple-element.26.ak, bf16[2,128,256]{2,1,0:T(8,128)(2,1)S(1)} %get-tuple-element.27.av), custom_call_target="tpu_custom_call" | custom-call | flops 1610612736 | bytes 12582912 | tf_op jit(solution)/shard_map/pallas_call | solution.py:392
  142.1 0.7 copy.50
  142.8 0.7 copy.51
  (23 shorter events, 0.9 us)
Async XLA Ops:
  2.1 73.5 %copy-start.4 = (bf16[1,1,32,4096]{3,2,1,0:T(8,128)(2,1)S(1)}, bf16[1,1,32,4096]{3,2,1,0:T(8,128)(2,1)}, u32[]{:S(2)}) copy-start(bf16[1,1,32,4096]{3,2,1,0:T(8,128)(2,1)} %param.8) | copy-start | bytes 786436
  2.1 85.0 %copy-start.1 = (bf16[1,1,32,4096]{3,2,1,0:T(8,128)(2,1)S(1)}, bf16[1,1,32,4096]{3,2,1,0:T(8,128)(2,1)}, u32[]{:S(2)}) copy-start(bf16[1,1,32,4096]{3,2,1,0:T(8,128)(2,1)} %param.9) | copy-start | bytes 786436
  75.6 14.8 %copy-start.3 = (bf16[128,1024]{1,0:T(8,128)(2,1)S(1)}, bf16[128,1024]{1,0:T(8,128)(2,1)}, u32[]{:S(2)}) copy-start(bf16[128,1024]{1,0:T(8,128)(2,1)} %get-tuple-element.22) | copy-start | bytes 786436
  76.8 65.3 %collective-permute-start = (bf16[32,4096]{1,0:T(8,128)(2,1)S(1)}, bf16[32,4096]{1,0:T(8,128)(2,1)S(1)}, u32[]{:S(2)}, u32[]{:S(2)}) collective-permute-start(bf16[32,4096]{1,0:T(8,128)(2,1)S(1)} %add_convert_fusion), channel_id=1, source_target_pairs={{0,8},{8,16},{16,24},{24,0},{1,9},{9,17},{17,25},{25,1},{2,10},{10... | collective-permute-start | bytes 786440 | tf_op jit(solution)/shard_map/ppermute | solution.py:20
  98.8 2.6 %copy-start.2 = (bf16[1,4096,256]{2,1,0:T(8,128)(2,1)S(1)}, bf16[1,4096,256]{2,1,0:T(8,128)(2,1)}, u32[]{:S(2)}) copy-start(bf16[1,4096,256]{2,1,0:T(8,128)(2,1)} %param.14) | copy-start | bytes 6291460
  102.3 31.5 %copy-start.5 = (bf16[1,1,32,4096]{3,2,1,0:T(8,128)(2,1)S(1)}, bf16[1,1,32,4096]{3,2,1,0:T(8,128)(2,1)}, u32[]{:S(2)}) copy-start(bf16[1,1,32,4096]{3,2,1,0:T(8,128)(2,1)} %param.10) | copy-start | bytes 786436
  133.5 1.3 copy-start
  134.0 8.1 %collective-permute-start.1 = (bf16[32,4096]{1,0:T(8,128)(2,1)S(1)}, bf16[32,4096]{1,0:T(8,128)(2,1)S(1)}, u32[]{:S(2)}, u32[]{:S(2)}) collective-permute-start(bf16[32,4096]{1,0:T(8,128)(2,1)S(1)} %fusion.27), channel_id=1, source_target_pairs={{0,24},{8,0},{16,8},{24,16},{1,25},{9,1},{17,9},{25,17},{2,26},{10... | collective-permute-start | bytes 786440 | tf_op jit(solution)/shard_map/ppermute | solution.py:20
